TPU v7x, 32 devices: a whole 2x2x4 slice. The times are simulated.
32 devices in a mesh: shard: 8 (over z, y), width: 4 (over x, core).
Axes of the slice: x: 2, y: 2, z: 4, core: 2. Of those that a mesh axis runs over, the one named last changes fastest.
Arguments:
- one_query: float32 [3584, 4096], P('shard', 'width'), may hold values from -0.125 to 0.125
- other_query: float32 [3584, 4096], P('shard', 'width'), may hold values from -0.09375 to 0.09375
- one_key: float32 [3584, 2048], P('shard', 'width'), may hold values from -0.125 to 0.125
- other_key: float32 [3584, 2048], P('shard', 'width'), may hold values from -0.09375 to 0.09375
- one_value: float32 [3584, 2048], P('shard', 'width'), may hold values from -0.125 to 0.125
- other_value: float32 [3584, 2048], P('shard', 'width'), may hold values from -0.09375 to 0.09375
- mix_share: float32 [3584], P('shard'), may hold values from 0.2 to 0.8
- norm_gain: float32 [3584], P('shard'), may hold values from 0.25 to 1.75
Outputs:
- final_query: bfloat16 [3584, 4096], P(None, 'width')
- final_key: bfloat16 [3584, 2048], P(None, 'width')
- final_value: bfloat16 [3584, 2048], P(None, 'width')
- scale_query: float32 [4096], P('width')
- scale_key: float32 [2048], P('width')
- scale_value: float32 [2048], P('width')
All inputs are finite; a program needn't handle non-finite values.
Results may differ from a plain program's by a relative error of at most 0.001.
Values may be sent and summed in bfloat16 or wider, within the bound.
A program may use at most 128 MiB of HBM per device.

v0:
```python
import jax
import jax.numpy as jnp
from jax import lax
from jax.sharding import PartitionSpec as P


def body(one_query, other_query, one_key, other_key, one_value, other_value, mix_share, norm_gain):
    result_query = mix_share[:, None] * one_query + (1.0 - mix_share[:, None]) * other_query
    result_key = mix_share[:, None] * one_key + (1.0 - mix_share[:, None]) * other_key
    result_value = mix_share[:, None] * one_value + (1.0 - mix_share[:, None]) * other_value
    result_gained_query = result_query * norm_gain[:, None]
    result_gained_key = result_key * norm_gain[:, None]
    result_gained_value = result_value * norm_gain[:, None]
    total_query, total_key, total_value = lax.psum(
        (
            jnp.sum(result_gained_query * result_gained_query, axis=0),
            jnp.sum(result_gained_key * result_gained_key, axis=0),
            jnp.sum(result_gained_value * result_gained_value, axis=0),
        ),
        "shard",
    )
    scale_query = jnp.sqrt(total_query)
    scale_key = jnp.sqrt(total_key)
    scale_value = jnp.sqrt(total_value)
    narrow_query, narrow_key, narrow_value = (
        (result_gained_query / scale_query).astype(jnp.bfloat16),
        (result_gained_key / scale_key).astype(jnp.bfloat16),
        (result_gained_value / scale_value).astype(jnp.bfloat16),
    )
    final_query, final_key, final_value = (
        lax.all_gather(narrow_query, "shard", axis=0, tiled=True),
        lax.all_gather(narrow_key, "shard", axis=0, tiled=True),
        lax.all_gather(narrow_value, "shard", axis=0, tiled=True),
    )
    return (final_query, final_key, final_value, scale_query, scale_key, scale_value)


def solution(mesh):
    return jax.shard_map(
        body,
        mesh=mesh,
        in_specs=(
            P("shard", "width"),
            P("shard", "width"),
            P("shard", "width"),
            P("shard", "width"),
            P("shard", "width"),
            P("shard", "width"),
            P("shard"),
            P("shard"),
        ),
        out_specs=(
            P(None, "width"),
            P(None, "width"),
            P(None, "width"),
            P("width"),
            P("width"),
            P("width"),
        ),
        check_vma=False,
    )
```

profile of v0, /device:TPU:0, one launch (start us, length us, event | category | flops | bytes accessed | tf_op | source)
XLA Modules:
  0.0 301.1 jit_solution(12646652363739461721)
XLA Ops:
  7.2 0.0 all-gather.6.cloned.1.call-start
  7.2 0.7 broadcast_subtract_fusion
  7.9 0.0 copy-start.2
  7.9 0.0 copy-start.3
  7.9 0.0 copy-start.4
  7.9 0.0 copy-start.5
  7.9 0.0 copy-start.6
  7.9 0.0 copy-start.8
  7.9 2.7 multiply_reduce_fusion
  10.6 0.0 copy-done.2
  10.6 0.0 copy-done.3
  10.6 0.1 copy-done.4
  10.8 0.3 copy-done.5
  11.0 0.0 copy-done.6
  11.0 0.0 copy-done.8
  11.0 1.4 multiply_reduce_fusion.1
  12.4 23.4 %all-reduce = (f32[1024]{0:T(1024)S(1)}, f32[512]{0:T(512)S(1)}, f32[512]{0:T(512)S(1)}) all-reduce(f32[1024]{0:T(1024)S(1)} %get-tuple-element.13, f32[512]{0:T(512)S(1)} %get-tuple-element.15, f32[512]{0:T(512)S(1)} %get-tuple-element.9), channel_id=1, replica_groups=mesh['shard'=8,'width'=4] {'shard'}, use_global_device_ids=true, to_apply=%region_1.0 | all-reduce | flops 2048 | bytes 16384 | tf_op jit(solution)/shard_map/psum | solution.py:14
  35.8 0.0 copy-start.9
  35.8 2.0 divide_convert_fusion.2
  37.9 0.0 all-gather.6.cloned.1.call-update
  37.9 0.0 all-gather.8.cloned.1.call-start
  38.0 0.0 copy-start.10
  38.0 0.9 divide_convert_fusion.1
  38.8 0.0 all-gather.8.cloned.1.call-update
  38.9 0.0 copy-done.9
  38.9 0.0 all-gather.4.cloned.1.call-start
  38.9 0.0 copy-start.7
  38.9 1.1 divide_convert_fusion
  40.1 0.0 copy-done.10
  40.1 0.0 all-gather.4.cloned.1.call-update
  40.1 0.0 copy-done.7
  40.1 61.4 %all-gather.6.cloned.1.call-done = bf16[3584,512]{1,0:T(8,128)(2,1)} async-done(((bf16[448,512]{1,0:T(8,128)(2,1)}), bf16[3584,512]{1,0:T(8,128)(2,1)}) %all-gather.6.cloned.1.call-update) | async-done | bytes 3670032 | tf_op jit(solution)/shard_map/all_gather | solution.py:32
  101.5 67.7 %all-gather.8.cloned.1.call-done = bf16[3584,512]{1,0:T(8,128)(2,1)} async-done(((bf16[448,512]{1,0:T(8,128)(2,1)}), bf16[3584,512]{1,0:T(8,128)(2,1)}) %all-gather.8.cloned.1.call-update) | async-done | bytes 3670032 | tf_op jit(solution)/shard_map/all_gather | solution.py:33
  169.2 113.0 %all-gather.4.cloned.1.call-done = bf16[3584,1024]{1,0:T(8,128)(2,1)} async-done(((bf16[448,1024]{1,0:T(8,128)(2,1)}), bf16[3584,1024]{1,0:T(8,128)(2,1)}) %all-gather.4.cloned.1.call-update) | async-done | bytes 7340048 | tf_op jit(solution)/shard_map/all_gather | solution.py:31
  282.2 0.0 copy-start
  282.2 7.1 %copy.17 = bf16[3584,1024]{1,0:T(8,128)(2,1)} copy(bf16[3584,1024]{1,0:T(8,128)(2,1)} %all-gather.4.cloned.1.call-done) | data formatting | bytes 14680064
  289.4 0.0 copy-done
  289.4 0.0 copy-start.1
  289.4 1.9 copy.18
  291.2 1.5 copy-done.1
  292.7 1.8 copy.19
  (3 shorter events, 0.0 us)
Async XLA Ops:
  7.2 94.3 %all-gather.6.cloned.1.call-start = ((), (), s32[]{:S(2)}) async-start(), calls=%async_computation.1 | async-start | bytes 4128768 | tf_op jit(solution)/shard_map/all_gather | solution.py:32
  7.9 2.7 copy-start.2
  7.9 2.7 copy-start.3
  7.9 2.8 copy-start.4
  7.9 3.1 %copy-start.5 = (f32[448,512]{1,0:T(8,128)S(1)}, f32[448,512]{1,0:T(8,128)}, u32[]{:S(2)}) copy-start(f32[448,512]{1,0:T(8,128)} %param.10) | copy-start | bytes 2752516
  7.9 3.1 %copy-start.6 = (f32[448]{0:T(512)S(1)}, f32[448]{0:T(512)}, u32[]{:S(2)}) copy-start(f32[448]{0:T(512)} %param.14) | copy-start | bytes 5380
  7.9 3.1 %copy-start.8 = (f32[448]{0:T(512)S(1)}, f32[448]{0:T(512)}, u32[]{:S(2)}) copy-start(f32[448]{0:T(512)} %param.15) | copy-start | bytes 5380
  35.8 3.1 %copy-start.9 = (f32[512]{0:T(512)}, f32[512]{0:T(512)S(1)}, u32[]{:S(2)}) copy-start(f32[512]{0:T(512)S(1)} %sqrt.10) | copy-start | bytes 6148
  37.9 131.3 %all-gather.8.cloned.1.call-start = ((), (), s32[]{:S(2)}) async-start(), calls=%async_computation.2 | async-start | bytes 4128768 | tf_op jit(solution)/shard_map/all_gather | solution.py:33
  38.0 2.1 copy-start.10
  38.9 243.4 %all-gather.4.cloned.1.call-start = ((), (), s32[]{:S(2)}) async-start(), calls=%async_computation | async-start | bytes 8257536 | tf_op jit(solution)/shard_map/all_gather | solution.py:31
  38.9 1.2 copy-start.7
  282.2 7.1 %copy-start = (bf16[3584,512]{1,0:T(8,128)(2,1)S(1)}, bf16[3584,512]{1,0:T(8,128)(2,1)}, u32[]{:S(2)}) copy-start(bf16[3584,512]{1,0:T(8,128)(2,1)} %all-gather.6.cloned.1.call-done) | copy-start | bytes 11010052
  289.4 3.4 %copy-start.1 = (bf16[3584,512]{1,0:T(8,128)(2,1)S(1)}, bf16[3584,512]{1,0:T(8,128)(2,1)}, u32[]{:S(2)}) copy-start(bf16[3584,512]{1,0:T(8,128)(2,1)} %all-gather.8.cloned.1.call-done) | copy-start | bytes 11010052
Sparse Core Ops, SparseCore 0:
  38.0 63.4 all-gather.5
  104.3 64.9 all-gather.7
  172.0 110.1 all-gather.3
where the time goes:
time: 301 us
  waiting for transfers between devices  242 us (80%)
  blocking collectives  23.4 us (8%)
  between operations  13.9 us (5%)
  local copies, waits for them, and re-layouts  12.8 us (4%)
  other arithmetic  8.81 us (3%)
    all_gather x1, waiting for transfers between devices, body(): lax.all_gather(narrow_query, 'shard', axis=0, tiled=True)  113 us
    all_gather x1, waiting for transfers between devices, body(): lax.all_gather(narrow_value, 'shard', axis=0, tiled=True)  67.7 us
    all_gather x1, waiting for transfers between devices, body(): lax.all_gather(narrow_key, 'shard', axis=0, tiled=True)  61.4 us
    psum x1, blocking collectives, body(): lax.psum((jnp.sum(result_gained_query * result_gained_query, axis=0), jnp...  23.4 us
    unnamed x25, local copies, waits for them, and re-layouts  12.8 us
  transfers between devices with their start and end apart: 3, of which 3 were waited for; matrix products, arithmetic and copies ran while one was open for 1% of the time, Pallas kernels for 0%

commit v1 on v0

--- a/solution.py
+++ b/solution.py
@@ -1,10 +1,17 @@
+import functools
+
 import jax
 import jax.numpy as jnp
 from jax import lax
+from jax.experimental import pallas as pl
+from jax.experimental.pallas import tpu as pltpu
 from jax.sharding import PartitionSpec as P
 
-
-def body(one_query, other_query, one_key, other_key, one_value, other_value, mix_share, norm_gain):
+MESH = pl.DeviceIdType.MESH
+ROWS = 16
+
+
+def plain(one_query, other_query, one_key, other_key, one_value, other_value, mix_share, norm_gain):
     result_query = mix_share[:, None] * one_query + (1.0 - mix_share[:, None]) * other_query
     result_key = mix_share[:, None] * one_key + (1.0 - mix_share[:, None]) * other_key
     result_value = mix_share[:, None] * one_value + (1.0 - mix_share[:, None]) * other_value
@@ -35,7 +42,223 @@
     return (final_query, final_key, final_value, scale_query, scale_key, scale_value)
 
 
+def cuts(blocks, parts):
+    edges = [blocks * part // parts for part in range(parts + 1)]
+    return [(low * ROWS, (high - low) * ROWS) for low, high in zip(edges, edges[1:])]
+
+
+def plan(rows, line):
+    blocks = rows // ROWS
+    far = max(1, round(blocks / (2 * (line - 1)))) if line > 1 else 0
+    pieces = cuts(blocks - far, 5)
+    near = len(pieces)
+    if far:
+        pieces.append(((blocks - far) * ROWS, far * ROWS))
+    return pieces, near
+
+
+def gather_kernel(n, widths, share_ref, gain_ref, *refs):
+    ins, (buf, scale_ref, first, second, sums, in_sem, sum_send, sum_recv, send_sem, recv_sem) = refs[:6], refs[6:]
+    rows = first.shape[0]
+    total = sum(widths)
+    line = n // 2
+    me = lax.axis_index("shard")
+    z, y = me // 2, me % 2
+    other = z * 2 + 1 - y
+    pieces, near = plan(rows, line)
+    starts = [sum(widths[:i]) for i in range(len(widths))]
+
+    loads = []
+    parts = cuts(rows // ROWS, 4)
+    for p, (low, size) in enumerate(parts):
+        group = []
+        for i, ref in enumerate(ins):
+            dest = (first, second)[i % 2].at[pl.ds(low, size), pl.ds(starts[i // 2], widths[i // 2])]
+            copy = pltpu.make_async_copy(ref.at[pl.ds(low, size), :], dest, in_sem.at[p, i])
+            copy.start()
+            group.append(copy)
+        loads.append(group)
+
+    barrier = pltpu.get_barrier_semaphore()
+    for step in range(1, n):
+        pl.semaphore_signal(barrier, inc=1, device_id={"shard": lax.rem(me + step, n)}, device_id_type=MESH)
+
+    def mixed(block, acc):
+        at = pl.ds(pl.multiple_of(block * ROWS, ROWS), ROWS)
+        share, gain = share_ref[at, :], gain_ref[at, :]
+        left, right = share * gain, (1.0 - share) * gain
+        out = []
+        for i in range(len(acc)):
+            cols = pl.ds(i * 512, 512)
+            value = left * first[at, cols] + right * second[at, cols]
+            first[at, cols] = value
+            square = value * value
+            out.append(acc[i] + square[:8] + square[8:])
+        return tuple(out)
+
+    acc = tuple(jnp.zeros((8, 512), jnp.float32) for _ in range(total // 512))
+    for group, (low, size) in zip(loads, parts):
+        for copy in group:
+            copy.wait()
+        acc = lax.fori_loop(low // ROWS, (low + size) // ROWS, mixed, acc)
+    for i, value in enumerate(acc):
+        sums[me, :, pl.ds(i * 512, 512)] = jnp.sum(value, axis=0, keepdims=True)
+
+    pl.semaphore_wait(barrier, n - 1)
+
+    def sum_copy(step, source):
+        return pltpu.make_async_remote_copy(
+            src_ref=sums.at[source], dst_ref=sums.at[source], send_sem=sum_send.at[step], recv_sem=sum_recv.at[source],
+            device_id={"shard": lax.rem(me + step, n)}, device_id_type=MESH)
+
+    for step in range(1, n):
+        sum_copy(step, me).start()
+    for step in range(1, n):
+        sum_copy(step, lax.rem(me + step, n)).wait_recv()
+    whole = sums[0]
+    for source in range(1, n):
+        whole = whole + sums[source]
+    scale = jnp.sqrt(whole)
+    scale_ref[...] = scale
+    inverse = jnp.broadcast_to(1.0 / scale, (8, total))
+
+    def copy(way, source, c):
+        low, size = pieces[c]
+        target = (jnp.minimum(z + 1, line - 1) * 2 + y, jnp.maximum(z - 1, 0) * 2 + y, other)[way]
+        ref = buf.at[source, pl.ds(low, size), :]
+        return pltpu.make_async_remote_copy(
+            src_ref=ref, dst_ref=ref, send_sem=send_sem.at[way, source, c], recv_sem=recv_sem.at[source, c],
+            device_id={"shard": target}, device_id_type=MESH)
+
+    sent = []
+
+    up, down = z < line - 1, z > 0
+
+    def scaled(block, carry):
+        at = pl.ds(pl.multiple_of(block * ROWS, ROWS), ROWS)
+        for i in range(total // 512):
+            cols = pl.ds(i * 512, 512)
+            wide = jnp.concatenate([inverse[:, i * 512:(i + 1) * 512]] * 2, axis=0)
+            buf[me, at, cols] = (first[at, cols] * wide).astype(buf.dtype)
+        return carry
+
+    def issue(condition, way, source, c):
+        @pl.when(condition)
+        def _():
+            copy(way, source, c).start()
+        sent.append((condition, way, source, c))
+
+    always = z >= 0
+
+    def issue_own(c):
+        issue(up, 0, me, c)
+        issue(down, 1, me, c)
+        issue(always, 2, me, c)
+
+    for c, (low, size) in enumerate(pieces):
+        lax.fori_loop(low // ROWS, (low + size) // ROWS, scaled, 0)
+        if c:
+            issue_own(c - 1)
+    issue_own(len(pieces) - 1)
+
+    def pass_on(condition, source, c, ways):
+        @pl.when(condition)
+        def _():
+            copy(2, source, c).wait_recv()
+        for extra, way in ways:
+            issue(condition & extra, way, source, c)
+
+    def relay(step):
+        for c in range(near, len(pieces)):
+            if step == 0:
+                pass_on(always, other, c, [(up, 0), (down, 1)])
+            else:
+                pass_on(z >= step, other - 2 * step, c, [(up, 0)])
+                pass_on(z + step < line, other + 2 * step, c, [(down, 1)])
+
+    for step in range(1, line):
+        for c in range(len(pieces)):
+            across = [(always, 2)] if c < near else []
+            pass_on(z >= step, me - 2 * step, c, [(up, 0)] + across)
+            pass_on(z + step < line, me + 2 * step, c, [(down, 1)] + across)
+        relay(step - 1)
+    relay(line - 1)
+    for c in range(near):
+        pass_on(always, other, c, [])
+    for step in range(1, line):
+        for c in range(near):
+            pass_on(z >= step, other - 2 * step, c, [])
+            pass_on(z + step < line, other + 2 * step, c, [])
+    for condition, way, source, c in sent:
+        @pl.when(condition)
+        def _():
+            copy(way, source, c).wait_send()
+    for step in range(1, n):
+        sum_copy(step, me).wait_send()
+
+
+def store_kernel(n, widths, buf, scale_ref, *refs):
+    outs, scales, sem = refs[:3], refs[3:6], refs[6]
+    rows = buf.shape[1]
+    copies = []
+    for source in range(n):
+        start = 0
+        for i, width in enumerate(widths):
+            copies.append(pltpu.make_async_copy(
+                buf.at[source, :, pl.ds(start, width)], outs[i].at[pl.ds(source * rows, rows), :], sem.at[source, i]))
+            copies[-1].start()
+            start += width
+    start = 0
+    for i, width in enumerate(widths):
+        scales[i][...] = scale_ref[:, start:start + width]
+        start += width
+    for copy in copies:
+        copy.wait()
+
+
+def routed(n, one_query, other_query, one_key, other_key, one_value, other_value, mix_share, norm_gain):
+    widths = (one_query.shape[1], one_key.shape[1], one_value.shape[1])
+    rows, total = one_query.shape[0], sum(widths)
+    pieces = len(plan(rows, n // 2)[0])
+    vmem = pl.BlockSpec(memory_space=pltpu.VMEM)
+    hbm = pl.BlockSpec(memory_space=pl.ANY)
+    buf, scale = pl.pallas_call(
+        functools.partial(gather_kernel, n, widths),
+        out_shape=(pltpu.VMEM((n, rows, total), jnp.bfloat16), pltpu.VMEM((1, total), jnp.float32)),
+        in_specs=[vmem] * 2 + [hbm] * 6,
+        out_specs=(vmem, vmem),
+        scratch_shapes=[
+            pltpu.VMEM((rows, total), jnp.float32),
+            pltpu.VMEM((rows, total), jnp.float32),
+            pltpu.VMEM((n, 1, total), jnp.float32),
+            pltpu.SemaphoreType.DMA((4, 6)),
+            pltpu.SemaphoreType.DMA((n,)),
+            pltpu.SemaphoreType.DMA((n,)),
+            pltpu.SemaphoreType.DMA((3, n, pieces)),
+            pltpu.SemaphoreType.DMA((n, pieces)),
+        ],
+        compiler_params=pltpu.CompilerParams(collective_id=0, has_side_effects=True, vmem_limit_bytes=44 * 2**20),
+    )(mix_share[:, None], norm_gain[:, None], one_query, other_query, one_key, other_key, one_value, other_value)
+    outs = pl.pallas_call(
+        functools.partial(store_kernel, n, widths),
+        out_shape=tuple(jax.ShapeDtypeStruct((n * rows, width), jnp.bfloat16) for width in widths)
+        + tuple(jax.ShapeDtypeStruct((1, width), jnp.float32) for width in widths),
+        in_specs=[vmem, vmem],
+        out_specs=(hbm,) * 3 + (vmem,) * 3,
+        scratch_shapes=[pltpu.SemaphoreType.DMA((n, 3))],
+        compiler_params=pltpu.CompilerParams(vmem_limit_bytes=2**20),
+    )(pltpu.with_memory_space_constraint(buf, pltpu.VMEM), pltpu.with_memory_space_constraint(scale, pltpu.VMEM))
+    return outs[:3] + tuple(out[0] for out in outs[3:])
+
+
 def solution(mesh):
+    n = mesh.shape["shard"]
+
+    def body(*args):
+        if n % 2 or n < 4 or args[0].shape[0] % ROWS or args[0].shape[0] < 6 * ROWS:
+            return plain(*args)
+        return routed(n, *args)
+
     return jax.shard_map(
         body,
         mesh=mesh,

time: 301 us -> 165 us (0.55)
  waiting for transfers between devices: 242 us -> 0 us
  Pallas kernels: 0 us -> 161 us
  blocking collectives: 23.4 us -> 0 us
  between operations: 13.9 us -> 0.64 us
  local copies, waits for them, and re-layouts: 12.8 us -> 3.02 us
  other arithmetic: 8.81 us -> 0 us
    all_gather x3 -> x0, waiting for transfers between devices: 242 us -> none  [the longest x1 113 us: body(): lax.all_gather(narrow_query, 'shard', axis=0, tiled=True)]
    pallas_call x0 -> x2, Pallas kernels: none -> 161 us  [the longest x1 155 us: routed(): pl.pallas_call(functools.partial(gather_kernel, n, widths), out_shape=(pl...]
    psum x1 -> x0, blocking collectives: 23.4 us -> none  [body(): lax.psum((jnp.sum(result_gained_query * result_gained_query, axis=0), jnp...]
    unnamed x25 -> x0, local copies, waits for them, and re-layouts: 12.8 us -> none
    convert_element_type x3 -> x0, other arithmetic: 4.07 us -> none  [the longest x1 2.05 us: body(): (result_gained_key / scale_key).astype(jnp.bfloat16)]
    reduce_sum x2 -> x0, other arithmetic: 4.06 us -> none  [the longest x1 2.68 us: body(): jnp.sum(result_gained_query * result_gained_query, axis=0)]
    broadcast_in_dim x0 -> x2, local copies, waits for them, and re-layouts: none -> 3.02 us  [the longest x1 1.51 us: routed(): mix_share[:, None]]
  transfers between devices with their start and end apart: 3 -> 0, of which waited for: 3 -> 0; matrix products, arithmetic and copies ran while one was open for 1% -> 0% of each run, Pallas kernels for 0% -> 0%
where the time goes in v1:
time: 165 us
  Pallas kernels  161 us (98%)
  local copies, waits for them, and re-layouts  3.02 us (2%)
    pallas_call x1, Pallas kernels, routed(): pl.pallas_call(functools.partial(gather_kernel, n, widths), out_shape=(pl...  155 us
    pallas_call x1, Pallas kernels, routed(): pl.pallas_call(functools.partial(store_kernel, n, widths), out_shape=tupl...  5.98 us

profile of v1, /device:TPU:0, one launch (start us, length us, event | category | flops | bytes accessed | tf_op | source)
XLA Modules:
  0.0 164.6 jit_solution(9267158387703660893)
XLA Ops:
  0.6 1.5 copy.14.share_ref
  2.1 1.5 copy.15.gain_ref
  3.7 155.0 %shard_map.127 = (bf16[8,448,2048]{2,1,0:T(8,128)(2,1)S(1)}, f32[1,2048]{1,0:T(1,128)S(1)}) custom-call(f32[448,1]{1,0:T(8,128)} %copy.14.share_ref, f32[448,1]{1,0:T(8,128)} %copy.15.gain_ref, f32[448,1024]{1,0:T(8,128)} %refs_0_.1, f32[448,1024]{1,0:T(8,128)} %refs_1_.1, f32[448,512]{1,0:T(8,128)} %refs_2_.1, f32[448,512]{1,0:T(8,128)} %refs_3_.1, ...), custom_call_target="tpu_custom_call" | custom-call | tf_op jit(solution)/shard_map/pallas_call | solution.py:225
  158.6 6.0 %shard_map.128 = (bf16[3584,1024]{1,0:T(8,128)(2,1)}, bf16[3584,512]{1,0:T(8,128)(2,1)}, bf16[3584,512]{1,0:T(8,128)(2,1)}, f32[1,1024]{1,0:T(1,128)}, f32[1,512]{1,0:T(1,128)}, /*index=5*/f32[1,512]{1,0:T(1,128)}) custom-call(bf16[8,448,2048]{2,1,0:T(8,128)(2,1)S(1)} %get-tuple-element.14.buf, f32[1,2048]{1,0:T(1,128)S(1)} %get-tuple-element.15.scale_ref), custom_call_target="tpu_custom_call" | custom-call | tf_op jit(solution)/shard_map/pallas_call | solution.py:242

commit v2 on v1

--- a/solution.py
+++ b/solution.py
@@ -9,6 +9,8 @@
 
 MESH = pl.DeviceIdType.MESH
 ROWS = 16
+TILE = 8
+LANES = 128
 
 
 def plain(one_query, other_query, one_key, other_key, one_value, other_value, mix_share, norm_gain):
@@ -42,23 +44,19 @@
     return (final_query, final_key, final_value, scale_query, scale_key, scale_value)
 
 
-def cuts(blocks, parts):
-    edges = [blocks * part // parts for part in range(parts + 1)]
-    return [(low * ROWS, (high - low) * ROWS) for low, high in zip(edges, edges[1:])]
+def cuts(start, end, parts, unit):
+    edges = [start + (end - start) // unit * part // parts * unit for part in range(parts)] + [end]
+    return [(low, high - low) for low, high in zip(edges, edges[1:])]
 
 
 def plan(rows, line):
-    blocks = rows // ROWS
-    far = max(1, round(blocks / (2 * (line - 1)))) if line > 1 else 0
-    pieces = cuts(blocks - far, 5)
-    near = len(pieces)
-    if far:
-        pieces.append(((blocks - far) * ROWS, far * ROWS))
-    return pieces, near
+    far = max(1, round(rows / (2 * (line - 1) * TILE))) * TILE
+    pieces = cuts(0, rows - far, 3, ROWS)
+    return pieces + [(rows - far, far)], len(pieces)
 
 
 def gather_kernel(n, widths, share_ref, gain_ref, *refs):
-    ins, (buf, scale_ref, first, second, sums, in_sem, sum_send, sum_recv, send_sem, recv_sem) = refs[:6], refs[6:]
+    ins, (buf, scale_ref, first, second, left, right, sums, in_sem, sum_send, sum_recv, send_sem, recv_sem) = refs[:6], refs[6:]
     rows = first.shape[0]
     total = sum(widths)
     line = n // 2
@@ -69,7 +67,7 @@
     starts = [sum(widths[:i]) for i in range(len(widths))]
 
     loads = []
-    parts = cuts(rows // ROWS, 4)
+    parts = cuts(0, rows, 4, ROWS)
     for p, (low, size) in enumerate(parts):
         group = []
         for i, ref in enumerate(ins):
@@ -83,14 +81,19 @@
     for step in range(1, n):
         pl.semaphore_signal(barrier, inc=1, device_id={"shard": lax.rem(me + step, n)}, device_id_type=MESH)
 
+    for low in range(0, rows, LANES):
+        size = min(LANES, rows - low)
+        share, gain = share_ref[:, low:low + size], gain_ref[:, low:low + size]
+        for ref, row in ((left, share * gain), (right, (1.0 - share) * gain)):
+            ref[pl.ds(low, size), :] = jnp.transpose(jnp.broadcast_to(row, (LANES, size)))
+
     def mixed(block, acc):
         at = pl.ds(pl.multiple_of(block * ROWS, ROWS), ROWS)
-        share, gain = share_ref[at, :], gain_ref[at, :]
-        left, right = share * gain, (1.0 - share) * gain
+        ours, theirs = (jnp.concatenate([ref[at, :]] * 4, axis=1) for ref in (left, right))
         out = []
         for i in range(len(acc)):
             cols = pl.ds(i * 512, 512)
-            value = left * first[at, cols] + right * second[at, cols]
+            value = ours * first[at, cols] + theirs * second[at, cols]
             first[at, cols] = value
             square = value * value
             out.append(acc[i] + square[:8] + square[8:])
@@ -155,8 +158,10 @@
         issue(down, 1, me, c)
         issue(always, 2, me, c)
 
+    done = 0
     for c, (low, size) in enumerate(pieces):
-        lax.fori_loop(low // ROWS, (low + size) // ROWS, scaled, 0)
+        lax.fori_loop(done, pl.cdiv(low + size, ROWS), scaled, 0)
+        done = pl.cdiv(low + size, ROWS)
         if c:
             issue_own(c - 1)
     issue_own(len(pieces) - 1)
@@ -230,6 +235,8 @@
         scratch_shapes=[
             pltpu.VMEM((rows, total), jnp.float32),
             pltpu.VMEM((rows, total), jnp.float32),
+            pltpu.VMEM((rows, LANES), jnp.float32),
+            pltpu.VMEM((rows, LANES), jnp.float32),
             pltpu.VMEM((n, 1, total), jnp.float32),
             pltpu.SemaphoreType.DMA((4, 6)),
             pltpu.SemaphoreType.DMA((n,)),
@@ -238,7 +245,7 @@
             pltpu.SemaphoreType.DMA((n, pieces)),
         ],
         compiler_params=pltpu.CompilerParams(collective_id=0, has_side_effects=True, vmem_limit_bytes=44 * 2**20),
-    )(mix_share[:, None], norm_gain[:, None], one_query, other_query, one_key, other_key, one_value, other_value)
+    )(mix_share[None, :], norm_gain[None, :], one_query, other_query, one_key, other_key, one_value, other_value)
     outs = pl.pallas_call(
         functools.partial(store_kernel, n, widths),
         out_shape=tuple(jax.ShapeDtypeStruct((n * rows, width), jnp.bfloat16) for width in widths)

time: 165 us -> 159 us (0.964)
  local copies, waits for them, and re-layouts: 3.02 us -> 0 us
  Pallas kernels: 161 us -> 158 us
    broadcast_in_dim x2 -> x0, local copies, waits for them, and re-layouts: 3.02 us -> none  [the longest x1 1.51 us: routed(): mix_share[:, None]]
    pallas_call x1, Pallas kernels: 155 us -> 152 us  [routed(): pl.pallas_call(functools.partial(gather_kernel, n, widths), out_shape=(pl...]
where the time goes in v2:
time: 159 us
  Pallas kernels  158 us (99%)
    pallas_call x1, Pallas kernels, routed(): pl.pallas_call(functools.partial(gather_kernel, n, widths), out_shape=(pl...  152 us
    pallas_call x1, Pallas kernels, routed(): pl.pallas_call(functools.partial(store_kernel, n, widths), out_shape=tupl...  5.98 us

profile of v2, /device:TPU:0, one launch (start us, length us, event | category | flops | bytes accessed | tf_op | source)
XLA Modules:
  0.0 159.0 jit_solution(4035893172753709680)
XLA Ops:
  0.6 152.3 %shard_map.127 = (bf16[8,448,2048]{2,1,0:T(8,128)(2,1)S(1)}, f32[1,2048]{1,0:T(1,128)S(1)}) custom-call(f32[1,448]{1,0:T(1,128)} %bitcast.5, f32[1,448]{1,0:T(1,128)} %bitcast.6, f32[448,1024]{1,0:T(8,128)} %refs_0_.1, f32[448,1024]{1,0:T(8,128)} %refs_1_.1, f32[448,512]{1,0:T(8,128)} %refs_2_.1, f32[448,512]{1,0:T(8,128)} %refs_3_.1, f32[448,512]{1,0:T(8,128)} %refs_4_.1, ...), custom_call_target="tpu_custom_call" | custom-call | tf_op jit(solution)/shard_map/pallas_call | solution.py:230
  153.0 6.0 %shard_map.128 = (bf16[3584,1024]{1,0:T(8,128)(2,1)}, bf16[3584,512]{1,0:T(8,128)(2,1)}, bf16[3584,512]{1,0:T(8,128)(2,1)}, f32[1,1024]{1,0:T(1,128)}, f32[1,512]{1,0:T(1,128)}, /*index=5*/f32[1,512]{1,0:T(1,128)}) custom-call(bf16[8,448,2048]{2,1,0:T(8,128)(2,1)S(1)} %get-tuple-element.14.buf, f32[1,2048]{1,0:T(1,128)S(1)} %get-tuple-element.15.scale_ref), custom_call_target="tpu_custom_call" | custom-call | tf_op jit(solution)/shard_map/pallas_call | solution.py:249

commit v3 on v2

--- a/solution.py
+++ b/solution.py
@@ -11,6 +11,7 @@
 ROWS = 16
 TILE = 8
 LANES = 128
+EARLY = ROWS
 
 
 def plain(one_query, other_query, one_key, other_key, one_value, other_value, mix_share, norm_gain):
@@ -51,12 +52,12 @@
 
 def plan(rows, line):
     far = max(1, round(rows / (2 * (line - 1) * TILE))) * TILE
-    pieces = cuts(0, rows - far, 3, ROWS)
+    pieces = [(0, EARLY)] + cuts(EARLY, rows - far, 2, ROWS)
     return pieces + [(rows - far, far)], len(pieces)
 
 
 def gather_kernel(n, widths, share_ref, gain_ref, *refs):
-    ins, (buf, scale_ref, first, second, left, right, sums, in_sem, sum_send, sum_recv, send_sem, recv_sem) = refs[:6], refs[6:]
+    ins, (buf, scale_ref, first, second, left, right, sums, early, in_sem, sum_send, sum_recv, early_send, early_recv, send_sem, recv_sem) = refs[:6], refs[6:]
     rows = first.shape[0]
     total = sum(widths)
     line = n // 2
@@ -109,15 +110,34 @@
 
     pl.semaphore_wait(barrier, n - 1)
 
-    def sum_copy(step, source):
+    def sum_copy(target, source):
         return pltpu.make_async_remote_copy(
-            src_ref=sums.at[source], dst_ref=sums.at[source], send_sem=sum_send.at[step], recv_sem=sum_recv.at[source],
-            device_id={"shard": lax.rem(me + step, n)}, device_id_type=MESH)
-
-    for step in range(1, n):
-        sum_copy(step, me).start()
-    for step in range(1, n):
-        sum_copy(step, lax.rem(me + step, n)).wait_recv()
+            src_ref=sums.at[source], dst_ref=sums.at[source], send_sem=sum_send.at[target], recv_sem=sum_recv.at[source],
+            device_id={"shard": target}, device_id_type=MESH)
+
+    peers = [jnp.where(z < line // 2, line - 1 - k, k) * 2 + side for k in range(line) for side in (1 - y, y)]
+    for peer in peers:
+        @pl.when(peer != me)
+        def _():
+            sum_copy(peer, me).start()
+
+    up, down, always = z < line - 1, z > 0, z >= 0
+    targets = (jnp.minimum(z + 1, line - 1) * 2 + y, jnp.maximum(z - 1, 0) * 2 + y, other)
+
+    def early_copy(way):
+        return pltpu.make_async_remote_copy(
+            src_ref=first.at[pl.ds(0, EARLY), :], dst_ref=early.at[way], send_sem=early_send.at[way],
+            recv_sem=early_recv.at[way], device_id={"shard": targets[way]}, device_id_type=MESH)
+
+    for way, condition in enumerate((up, down, always)):
+        @pl.when(condition)
+        def _():
+            early_copy(way).start()
+
+    for peer in peers:
+        @pl.when(peer != me)
+        def _():
+            sum_copy(other, peer).wait_recv()
     whole = sums[0]
     for source in range(1, n):
         whole = whole + sums[source]
@@ -127,31 +147,28 @@
 
     def copy(way, source, c):
         low, size = pieces[c]
-        target = (jnp.minimum(z + 1, line - 1) * 2 + y, jnp.maximum(z - 1, 0) * 2 + y, other)[way]
         ref = buf.at[source, pl.ds(low, size), :]
         return pltpu.make_async_remote_copy(
             src_ref=ref, dst_ref=ref, send_sem=send_sem.at[way, source, c], recv_sem=recv_sem.at[source, c],
-            device_id={"shard": target}, device_id_type=MESH)
+            device_id={"shard": targets[way]}, device_id_type=MESH)
 
     sent = []
 
-    up, down = z < line - 1, z > 0
-
-    def scaled(block, carry):
-        at = pl.ds(pl.multiple_of(block * ROWS, ROWS), ROWS)
-        for i in range(total // 512):
-            cols = pl.ds(i * 512, 512)
-            wide = jnp.concatenate([inverse[:, i * 512:(i + 1) * 512]] * 2, axis=0)
-            buf[me, at, cols] = (first[at, cols] * wide).astype(buf.dtype)
-        return carry
+    def scaled(source, ref):
+        def step(block, carry):
+            at = pl.ds(pl.multiple_of(block * ROWS, ROWS), ROWS)
+            for i in range(total // 512):
+                cols = pl.ds(i * 512, 512)
+                wide = jnp.concatenate([inverse[:, i * 512:(i + 1) * 512]] * 2, axis=0)
+                buf[source, at, cols] = (ref[at, cols] * wide).astype(buf.dtype)
+            return carry
+        return step
 
     def issue(condition, way, source, c):
         @pl.when(condition)
         def _():
             copy(way, source, c).start()
         sent.append((condition, way, source, c))
-
-    always = z >= 0
 
     def issue_own(c):
         issue(up, 0, me, c)
@@ -160,11 +177,21 @@
 
     done = 0
     for c, (low, size) in enumerate(pieces):
-        lax.fori_loop(done, pl.cdiv(low + size, ROWS), scaled, 0)
+        lax.fori_loop(done, pl.cdiv(low + size, ROWS), scaled(me, first), 0)
         done = pl.cdiv(low + size, ROWS)
-        if c:
+        if c > 1:
             issue_own(c - 1)
     issue_own(len(pieces) - 1)
+
+    for way, (condition, source) in enumerate(((down, me - 2), (up, me + 2), (always, other))):
+        @pl.when(condition)
+        def _():
+            early_copy(way).wait_recv()
+            lax.fori_loop(0, EARLY // ROWS, scaled(source, early.at[way]), 0)
+    issue(down & up, 0, me - 2, 0)
+    issue(down, 2, me - 2, 0)
+    issue(up & down, 1, me + 2, 0)
+    issue(up, 2, me + 2, 0)
 
     def pass_on(condition, source, c, ways):
         @pl.when(condition)
@@ -182,13 +209,13 @@
                 pass_on(z + step < line, other + 2 * step, c, [(down, 1)])
 
     for step in range(1, line):
-        for c in range(len(pieces)):
+        for c in range(1 if step == 1 else 0, len(pieces)):
             across = [(always, 2)] if c < near else []
             pass_on(z >= step, me - 2 * step, c, [(up, 0)] + across)
             pass_on(z + step < line, me + 2 * step, c, [(down, 1)] + across)
         relay(step - 1)
     relay(line - 1)
-    for c in range(near):
+    for c in range(1, near):
         pass_on(always, other, c, [])
     for step in range(1, line):
         for c in range(near):
@@ -198,8 +225,14 @@
         @pl.when(condition)
         def _():
             copy(way, source, c).wait_send()
-    for step in range(1, n):
-        sum_copy(step, me).wait_send()
+    for way, condition in enumerate((up, down, always)):
+        @pl.when(condition)
+        def _():
+            early_copy(way).wait_send()
+    for peer in peers:
+        @pl.when(peer != me)
+        def _():
+            sum_copy(peer, me).wait_send()
 
 
 def store_kernel(n, widths, buf, scale_ref, *refs):
@@ -238,9 +271,12 @@
             pltpu.VMEM((rows, LANES), jnp.float32),
             pltpu.VMEM((rows, LANES), jnp.float32),
             pltpu.VMEM((n, 1, total), jnp.float32),
+            pltpu.VMEM((3, EARLY, total), jnp.float32),
             pltpu.SemaphoreType.DMA((4, 6)),
             pltpu.SemaphoreType.DMA((n,)),
             pltpu.SemaphoreType.DMA((n,)),
+            pltpu.SemaphoreType.DMA((3,)),
+            pltpu.SemaphoreType.DMA((3,)),
             pltpu.SemaphoreType.DMA((3, n, pieces)),
             pltpu.SemaphoreType.DMA((n, pieces)),
         ],

time: 159 us -> 158 us (level)
  no operation moved by 1% of the time
where the time goes in v3:
time: 158 us
  Pallas kernels  157 us (99%)
    pallas_call x1, Pallas kernels, routed(): pl.pallas_call(functools.partial(gather_kernel, n, widths), out_shape=(pl...  151 us
    pallas_call x1, Pallas kernels, routed(): pl.pallas_call(functools.partial(store_kernel, n, widths), out_shape=tupl...  5.98 us

profile of v3, /device:TPU:0, one launch (start us, length us, event | category | flops | bytes accessed | tf_op | source)
XLA Modules:
  0.0 157.8 jit_solution(9271417218500321119)
XLA Ops:
  0.6 151.2 %shard_map.127 = (bf16[8,448,2048]{2,1,0:T(8,128)(2,1)S(1)}, f32[1,2048]{1,0:T(1,128)S(1)}) custom-call(f32[1,448]{1,0:T(1,128)} %bitcast.5, f32[1,448]{1,0:T(1,128)} %bitcast.6, f32[448,1024]{1,0:T(8,128)} %refs_0_.1, f32[448,1024]{1,0:T(8,128)} %refs_1_.1, f32[448,512]{1,0:T(8,128)} %refs_2_.1, f32[448,512]{1,0:T(8,128)} %refs_3_.1, f32[448,512]{1,0:T(8,128)} %refs_4_.1, ...), custom_call_target="tpu_custom_call" | custom-call | tf_op jit(solution)/shard_map/pallas_call | solution.py:263
  151.8 6.0 %shard_map.128 = (bf16[3584,1024]{1,0:T(8,128)(2,1)}, bf16[3584,512]{1,0:T(8,128)(2,1)}, bf16[3584,512]{1,0:T(8,128)(2,1)}, f32[1,1024]{1,0:T(1,128)}, f32[1,512]{1,0:T(1,128)}, /*index=5*/f32[1,512]{1,0:T(1,128)}) custom-call(bf16[8,448,2048]{2,1,0:T(8,128)(2,1)S(1)} %get-tuple-element.14.buf, f32[1,2048]{1,0:T(1,128)S(1)} %get-tuple-element.15.scale_ref), custom_call_target="tpu_custom_call" | custom-call | tf_op jit(solution)/shard_map/pallas_call | solution.py:285
